TPU v7x, 128 devices: a whole 4x4x4 slice. The times are simulated.
128 devices in a mesh: row: 8 (over y, z_lo), col: 16 (over z_hi, x, core).
Axes of the slice: x: 4, y: 4, z: 4 (z_hi: 2, z_lo: 2; z = z_hi * 2 + z_lo), core: 2. Of those that a mesh axis runs over, the one named last changes fastest.
Arguments:
- spectra: bfloat16 [16, 2048, 2048], P('row', None, 'col'), may hold values from -6 to 6
- coupling: float32 [16], replicated, may hold values from 0.2 to 1
Outputs:
- returned_spectra: bfloat16 [16, 2048, 2048], P('row', None, 'col')
All inputs are finite; a program needn't handle non-finite values.
Results may differ from a plain program's by a relative error of at most 0.0079.
Values may be sent and summed in bfloat16 or wider, within the bound.
A program may use at most 128 MiB of HBM per device.

v0:
```python
import math
import jax
import jax.numpy as jnp
from jax import lax
from jax.sharding import Mesh
from jax.sharding import PartitionSpec as P

NX = 3072
NY = 3072
M = 1024
COL = ("col_0", "col_1", "col_2")


def in_blocks(array, dim, peers):
    dims = array.shape
    tiles = array.reshape(*dims[:dim], peers, dims[dim] // peers, *dims[dim + 1 :])
    return jnp.moveaxis(tiles, dim, 0)


def joined_along(tiles, dim):
    dims = list(tiles.shape[1:])
    dims[dim] *= tiles.shape[0]
    return jnp.moveaxis(tiles, 0, dim).reshape(dims)


def moved_by_axis(tiles, axes, turns):
    dims = [lax.axis_size(a) for a in axes]
    tiles = tiles.reshape(*dims, *tiles.shape[1:])
    for k in turns:
        tiles = lax.all_to_all(tiles, axes[k], split_axis=k, concat_axis=k, tiled=True)
    return tiles.reshape(-1, *tiles.shape[len(axes) :])


def core_and_chips(array, groups, turns, split_dim, concat_dim):
    peers = lax.axis_size(groups[0]) * lax.axis_size(groups[1])
    tiles = in_blocks(array, split_dim, peers)
    return joined_along(moved_by_axis(tiles, groups, turns), concat_dim)


def fourier_rows(mode_count, length, factor):
    wavenumber = jnp.arange(1, mode_count + 1, dtype=jnp.int32)
    position = jnp.arange(length, dtype=jnp.int32)
    residue = wavenumber[:, None] * position[None, :] % length
    angles = residue.astype(jnp.float32) * (2.0 * math.pi / length)
    table = jnp.concatenate([jnp.cos(angles), jnp.sin(angles)], 0) * factor
    return table.astype(jnp.bfloat16)


def ellipse(row_index, column_index, mode_count):
    row_waves = row_index % mode_count + 1
    col_waves = column_index % mode_count + 1
    inside = (
        row_waves[:, None] * row_waves[:, None] + col_waves[None, :] * col_waves[None, :]
        <= mode_count * mode_count
    )
    return inside.astype(jnp.float32)


def on_device(spectra, coupling):
    local_count = spectra.shape[0]
    width_here = spectra.shape[2]
    inverse_y = fourier_rows(M, NY, 1.0 / math.sqrt(M)).T
    inverse_x = fourier_rows(M, NX, 1.0 / math.sqrt(M))
    forward_x = fourier_rows(M, NX, 2.0 * math.sqrt(M) / NX).T
    forward_y = fourier_rows(M, NY, 2.0 * math.sqrt(M) / NY)
    half_done = jnp.einsum(
        "yk,fkc->fyc", inverse_y, spectra, preferred_element_type=jnp.float32
    ).astype(jnp.bfloat16)
    gathered = core_and_chips(half_done, (("col_0", "col_1"), "col_2"), (1, 0), 1, 2)
    first_field = lax.axis_index("row") * local_count
    strength = lax.dynamic_slice_in_dim(coupling, first_field, gathered.shape[0])
    gridded = jnp.einsum("fyk,kx->fyx", gathered, inverse_x, preferred_element_type=jnp.float32)
    tendency = (gridded + strength[:, None, None] * gridded * gridded).astype(jnp.bfloat16)
    projected = jnp.einsum(
        "fyx,xk->fyk", tendency, forward_x, preferred_element_type=jnp.float32
    ).astype(jnp.bfloat16)
    returned = lax.all_to_all(projected, COL, split_axis=2, concat_axis=1, tiled=True)
    result = jnp.einsum("ky,fyc->fkc", forward_y, returned, preferred_element_type=jnp.float32)
    columns = lax.axis_index(COL) * width_here + jnp.arange(width_here, dtype=jnp.int32)
    inside = ellipse(jnp.arange(2 * M, dtype=jnp.int32), columns, M)
    return (result * inside[None, :, :]).astype(jnp.bfloat16)


def solution(mesh):
    torus = Mesh(
        mesh.devices.reshape(mesh.shape["row"], 2, 4, 2), ("row", "col_0", "col_1", "col_2")
    )
    return jax.shard_map(
        on_device,
        mesh=torus,
        in_specs=(P("row", None, COL), P()),
        out_specs=P("row", None, COL),
        check_vma=False,
    )
```

profile of v0, /device:TPU:1, one launch (start us, length us, event | category | flops | bytes accessed | tf_op | source)
XLA Modules:
  0.0 182.3 jit_solution(15126641113345682228)
XLA Ops:
  0.0 0.0 copy-start
  0.0 52.6 %fusion.7 = (f32[1024,3072]{0,1:T(8,128)}, f32[1024,3072]{0,1:T(8,128)}) fusion(s32[1024]{0:T(1024)S(1)} %iota_add_fusion), kind=kLoop, calls=%fused_computation.12 | loop fusion | flops 28311552 | bytes 25169920 | tf_op jit(solution)/shard_map/cos | solution.py:45
  52.6 0.0 copy-done
  52.6 10.0 %convolution_convert_fusion = bf16[3072,2,128]{2,0,1:T(8,128)(2,1)S(1)} fusion(bf16[2,2048,128]{2,1,0:T(8,128)(2,1)S(1)} %copy-done, f32[1024,3072]{0,1:T(8,128)} %get-tuple-element.6, f32[1024,3072]{0,1:T(8,128)} %get-tuple-element.5), kind=kOutput, calls=%fused_computation.16 | convolution fusion | flops 3240886272 | bytes 27787264 | tf_op jit(solution)/shard_map/yk,fkc->fyc/dot_general | solution.py:66
  62.6 0.0 copy-start.1
  62.6 0.1 copy.24
  62.8 6.0 %all_to_all.28 = bf16[8,2,2,192,128]{4,3,0,2,1:T(8,128)(2,1)S(1)} all-to-all(bf16[8,2,2,192,128]{4,3,0,2,1:T(8,128)(2,1)S(1)} %copy.24), channel_id=1, replica_groups=mesh['row'=8,'col_0'=2,'col_1'=4,'col_2'=2] {'col_2'}, dimensions={1} | all-to-all | bytes 3145728 | tf_op jit(solution)/shard_map/all_to_all | solution.py:30
  68.8 1.3 copy.25
  70.1 7.4 %all-to-all-start.1 = ((bf16[8,2,2,192,128]{4,3,1,2,0:T(8,128)(2,1)}), bf16[8,2,2,192,128]{4,3,1,2,0:T(8,128)(2,1)S(1)}, u32[]{:S(2)}, u32[]{:S(2)}) async-start(bf16[8,2,2,192,128]{4,3,1,2,0:T(8,128)(2,1)} %copy.25), calls=%async_computation.1 | async-start | bytes 3145728 | tf_op jit(solution)/shard_map/all_to_all | solution.py:30
  77.6 0.0 copy-done.1
  77.6 0.1 dynamic_slice.3
  77.7 22.9 %all-to-all-done.1 = bf16[8,2,2,192,128]{4,3,1,2,0:T(8,128)(2,1)S(1)} async-done(((bf16[8,2,2,192,128]{4,3,1,2,0:T(8,128)(2,1)}), bf16[8,2,2,192,128]{4,3,1,2,0:T(8,128)(2,1)S(1)}, u32[]{:S(2)}, u32[]{:S(2)}) %all-to-all-start.1) | async-done | bytes 1572896 | tf_op jit(solution)/shard_map/all_to_all | solution.py:30
  100.6 1.3 copy.26
  101.8 12.3 %fusion.9 = bf16[2,192,3072]{2,1,0:T(8,128)(2,1)} fusion(f32[2]{0:T(128)S(1)} %dynamic_slice.3, f32[1024,3072]{0,1:T(8,128)} %get-tuple-element.6, f32[1024,3072]{0,1:T(8,128)} %get-tuple-element.5, bf16[16,2,24,8,128]{4,3,2,1,0:T(8,128)(2,1)} %bitcast.40), kind=kOutput, calls=%fused_computation.15 | convolution fusion | flops 4855431168 | bytes 29097992 | tf_op jit(solution)/shard_map/fyk,kx->fyx/dot_general | solution.py:72
  114.1 13.9 %convolution_convert_fusion.1 = bf16[2,192,2048]{2,1,0:T(8,128)(2,1)S(1)} fusion(bf16[2,192,3072]{2,1,0:T(8,128)(2,1)} %fusion.9, f32[1024,3072]{0,1:T(8,128)} %get-tuple-element.6, f32[1024,3072]{0,1:T(8,128)} %get-tuple-element.5), kind=kOutput, calls=%fused_computation.17 | convolution fusion | flops 4851499008 | bytes 29097984 | tf_op jit(solution)/shard_map/fyx,xk->fyk/dot_general | solution.py:74
  128.1 3.8 %copy.30 = bf16[2,192,2048]{1,0,2:T(2,128)(2,1)} copy(bf16[2,192,2048]{2,1,0:T(8,128)(2,1)S(1)} %convolution_convert_fusion.1) | data formatting | bytes 3145728 | tf_op jit(solution)/shard_map/convert_element_type | solution.py:76
  131.9 4.6 %all-to-all-start.2 = ((bf16[2,192,2048]{1,0,2:T(2,128)(2,1)}), bf16[2,192,2048]{1,0,2:T(2,128)(2,1)S(1)}, u32[]{:S(2)}, u32[]{:S(2)}) async-start(bf16[2,192,2048]{1,0,2:T(2,128)(2,1)} %copy.30), calls=%async_computation.2 | async-start | bytes 4194304 | tf_op jit(solution)/shard_map/all_to_all | solution.py:77
  136.5 1.1 fusion.18
  137.7 27.3 %all-to-all-done.2 = bf16[2,192,2048]{1,0,2:T(2,128)(2,1)S(1)} async-done(((bf16[2,192,2048]{1,0,2:T(2,128)(2,1)}), bf16[2,192,2048]{1,0,2:T(2,128)(2,1)S(1)}, u32[]{:S(2)}, u32[]{:S(2)}) %all-to-all-start.2) | async-done | bytes 1572896 | tf_op jit(solution)/shard_map/all_to_all | solution.py:77
  165.0 3.7 %copy.44 = bf16[2,192,16,128]{3,1,2,0:T(8,128)(2,1)} copy(bf16[2,192,16,128]{1,0,3,2:T(2,128)(2,1)S(1)} %bitcast.38) | data formatting | bytes 3145728 | tf_op jit(solution)/shard_map/all_to_all | solution.py:77
  168.7 12.3 %fusion.11 = bf16[2,2048,128]{1,2,0:T(8,128)(2,1)S(1)} fusion(bf16[2,3072,128]{2,1,0:T(8,128)(2,1)} %bitcast.39, f32[1024,3072]{0,1:T(8,128)} %get-tuple-element.6, f32[1024,3072]{0,1:T(8,128)} %get-tuple-element.5, f32[2048,128]{0,1:T(8,128)} %fusion.18), kind=kOutput, calls=%fused_computation.20 | convolution fusion | flops 3241148416 | bytes 28835840 | tf_op jit(solution)/shard_map/ky,fyc->fkc/dot_general | solution.py:78
  181.0 1.3 copy.35
  (3 shorter events, 0.0 us)
Async XLA Ops:
  0.0 52.6 %copy-start = (bf16[2,2048,128]{2,1,0:T(8,128)(2,1)S(1)}, bf16[2,2048,128]{2,1,0:T(8,128)(2,1)}, u32[]{:S(2)}) copy-start(bf16[2,2048,128]{2,1,0:T(8,128)(2,1)} %param.2) | copy-start | bytes 3145732
  62.6 14.9 %copy-start.1 = (f32[16]{0:T(128)S(1)}, f32[16]{0:T(128)}, u32[]{:S(2)}) copy-start(f32[16]{0:T(128)} %param.3) | copy-start | bytes 196
  70.1 30.4 %all-to-all-start.1 = ((bf16[8,2,2,192,128]{4,3,1,2,0:T(8,128)(2,1)}), bf16[8,2,2,192,128]{4,3,1,2,0:T(8,128)(2,1)S(1)}, u32[]{:S(2)}, u32[]{:S(2)}) async-start(bf16[8,2,2,192,128]{4,3,1,2,0:T(8,128)(2,1)} %copy.25), calls=%async_computation.1 | async-start | bytes 3145728 | tf_op jit(solution)/shard_map/all_to_all | solution.py:30
  131.9 33.1 %all-to-all-start.2 = ((bf16[2,192,2048]{1,0,2:T(2,128)(2,1)}), bf16[2,192,2048]{1,0,2:T(2,128)(2,1)S(1)}, u32[]{:S(2)}, u32[]{:S(2)}) async-start(bf16[2,192,2048]{1,0,2:T(2,128)(2,1)} %copy.30), calls=%async_computation.2 | async-start | bytes 4194304 | tf_op jit(solution)/shard_map/all_to_all | solution.py:77
where the time goes:
time: 183 us; the launch traced here: 182 us
  other arithmetic  53.8 us (29%)
  waiting for transfers between devices  50.2 us (27%)
  matrix products  48.6 us (27%)
  starting transfers between devices  12.1 us (7%)
  local copies, waits for them, and re-layouts  11.6 us (6%)
  blocking collectives  6 us (3%)
    cos x1, other arithmetic, fourier_rows(): table = jnp.concatenate([jnp.cos(angles), jnp.sin(angles)], 0) * factor  52.6 us
    all_to_all x1, waiting for transfers between devices, on_device(): lax.all_to_all(projected, COL, split_axis=2, concat_axis=1, tiled=True)  27.3 us
    all_to_all x1, waiting for transfers between devices, moved_by_axis(): lax.all_to_all(tiles, axes[k], split_axis=k, concat_axis=k, tiled=True)  22.9 us
    dot_general x1, matrix products, on_device(): jnp.einsum('fyx,xk->fyk', tendency, forward_x, preferred_element_type=jnp...  13.9 us
    dot_general x1, matrix products, on_device(): jnp.einsum('fyk,kx->fyx', gathered, inverse_x, preferred_element_type=jnp...  12.3 us
    dot_general x1, matrix products, on_device(): jnp.einsum('ky,fyc->fkc', forward_y, returned, preferred_element_type=jnp...  12.3 us
    dot_general x1, matrix products, on_device(): jnp.einsum('yk,fkc->fyc', inverse_y, spectra, preferred_element_type=jnp....  10 us
    all_to_all x1, starting transfers between devices, moved_by_axis(): lax.all_to_all(tiles, axes[k], split_axis=k, concat_axis=k, tiled=True)  7.45 us
  transfers between devices with their start and end apart: 2, of which 2 were waited for; matrix products, arithmetic and copies ran while one was open for 1% of the time, Pallas kernels for 0%

commit v1 on v0

--- a/solution.py
+++ b/solution.py
@@ -4,6 +4,7 @@
 from jax import lax
 from jax.sharding import Mesh
 from jax.sharding import PartitionSpec as P
+from jax.lax import all_to_all, axis_size
 
 NX = 3072
 NY = 3072
@@ -74,7 +75,15 @@
     projected = jnp.einsum(
         "fyx,xk->fyk", tendency, forward_x, preferred_element_type=jnp.float32
     ).astype(jnp.bfloat16)
-    returned = lax.all_to_all(projected, COL, split_axis=2, concat_axis=1, tiled=True)
+
+    def _expand_widths(mine, named_axis):
+        local_part = axis_size(named_axis)
+        long_array = jnp.split(mine, local_part, 2)
+        met_up = jnp.stack(long_array)
+        tmp = all_to_all(met_up, named_axis, 0, 0)
+        return jnp.concatenate(tmp, axis=1)
+
+    returned = _expand_widths(projected, COL)
     result = jnp.einsum("ky,fyc->fkc", forward_y, returned, preferred_element_type=jnp.float32)
     columns = lax.axis_index(COL) * width_here + jnp.arange(width_here, dtype=jnp.int32)
     inside = ellipse(jnp.arange(2 * M, dtype=jnp.int32), columns, M)

time: 183 us -> 182 us (level)
  waiting for transfers between devices: 50.2 us -> 44.6 us
  local copies, waits for them, and re-layouts: 11.6 us -> 16.1 us
    unnamed x4 -> x19, local copies, waits for them, and re-layouts: 0.01 us -> 9.99 us
    all_to_all x1, waiting for transfers between devices: 27.3 us -> 21.7 us  [_expand_widths(): tmp = all_to_all(met_up, named_axis, 0, 0)]
    convert_element_type x1 -> x0, local copies, waits for them, and re-layouts: 3.83 us -> none  [on_device(): projected = jnp.einsum('fyx,xk->fyk', tendency, forward_x, preferred_elem...]
    all_to_all x1 -> x0, local copies, waits for them, and re-layouts: 3.66 us -> none  [on_device(): lax.all_to_all(projected, COL, split_axis=2, concat_axis=1, tiled=True)]
where the time goes in v1:
time: 182 us; the launch traced here: 181 us
  other arithmetic  53.8 us (30%)
  matrix products  48.6 us (27%)
  waiting for transfers between devices  44.6 us (25%)
  local copies, waits for them, and re-layouts  16.1 us (9%)
  starting transfers between devices  12.2 us (7%)
  blocking collectives  6 us (3%)
    cos x1, other arithmetic, fourier_rows(): table = jnp.concatenate([jnp.cos(angles), jnp.sin(angles)], 0) * factor  52.6 us
    all_to_all x1, waiting for transfers between devices, moved_by_axis(): lax.all_to_all(tiles, axes[k], split_axis=k, concat_axis=k, tiled=True)  22.9 us
    all_to_all x1, waiting for transfers between devices, _expand_widths(): tmp = all_to_all(met_up, named_axis, 0, 0)  21.7 us
    dot_general x1, matrix products, on_device(): jnp.einsum('fyx,xk->fyk', tendency, forward_x, preferred_element_type=jnp...  13.9 us
    dot_general x1, matrix products, on_device(): jnp.einsum('fyk,kx->fyx', gathered, inverse_x, preferred_element_type=jnp...  12.3 us
    dot_general x1, matrix products, on_device(): jnp.einsum('ky,fyc->fkc', forward_y, returned, preferred_element_type=jnp...  12.3 us
    dot_general x1, matrix products, on_device(): jnp.einsum('yk,fkc->fyc', inverse_y, spectra, preferred_element_type=jnp....  10 us
    unnamed x19, local copies, waits for them, and re-layouts  9.99 us
  transfers between devices with their start and end apart: 2, of which 2 were waited for; matrix products, arithmetic and copies ran while one was open for 1% of the time, Pallas kernels for 0%

profile of v1, /device:TPU:1, one launch (start us, length us, event | category | flops | bytes accessed | tf_op | source)
XLA Modules:
  0.0 181.3 jit_solution(3998821557926078322)
XLA Ops:
  0.0 0.0 copy-start
  0.0 52.6 %fusion.7 = (f32[1024,3072]{0,1:T(8,128)}, f32[1024,3072]{0,1:T(8,128)}) fusion(s32[1024]{0:T(1024)S(1)} %iota_add_fusion), kind=kLoop, calls=%fused_computation.12 | loop fusion | flops 28311552 | bytes 25169920 | tf_op jit(solution)/shard_map/cos | solution.py:46
  52.6 0.0 copy-done
  52.6 10.0 %convolution_convert_fusion = bf16[3072,2,128]{2,0,1:T(8,128)(2,1)S(1)} fusion(bf16[2,2048,128]{2,1,0:T(8,128)(2,1)S(1)} %copy-done, f32[1024,3072]{0,1:T(8,128)} %get-tuple-element.6, f32[1024,3072]{0,1:T(8,128)} %get-tuple-element.5), kind=kOutput, calls=%fused_computation.16 | convolution fusion | flops 3240886272 | bytes 27787264 | tf_op jit(solution)/shard_map/yk,fkc->fyc/dot_general | solution.py:67
  62.6 0.1 copy.23
  62.8 6.0 %all_to_all.15 = bf16[8,2,2,192,128]{4,3,0,2,1:T(8,128)(2,1)S(1)} all-to-all(bf16[8,2,2,192,128]{4,3,0,2,1:T(8,128)(2,1)S(1)} %copy.23), channel_id=1, replica_groups=mesh['row'=8,'col_0'=2,'col_1'=4,'col_2'=2] {'col_2'}, dimensions={1} | all-to-all | bytes 3145728 | tf_op jit(solution)/shard_map/all_to_all | solution.py:31
  68.8 1.3 copy.24
  70.1 0.0 copy-start.1
  70.1 7.6 %all-to-all-start.1 = ((bf16[8,2,2,192,128]{4,3,1,2,0:T(8,128)(2,1)}), bf16[8,2,2,192,128]{4,3,1,2,0:T(8,128)(2,1)S(1)}, u32[]{:S(2)}, u32[]{:S(2)}) async-start(bf16[8,2,2,192,128]{4,3,1,2,0:T(8,128)(2,1)} %copy.24), calls=%async_computation.1 | async-start | bytes 3145728 | tf_op jit(solution)/shard_map/all_to_all | solution.py:31
  77.7 0.0 copy-done.1
  77.7 0.1 dynamic_slice.3
  77.8 22.9 %all-to-all-done.1 = bf16[8,2,2,192,128]{4,3,1,2,0:T(8,128)(2,1)S(1)} async-done(((bf16[8,2,2,192,128]{4,3,1,2,0:T(8,128)(2,1)}), bf16[8,2,2,192,128]{4,3,1,2,0:T(8,128)(2,1)S(1)}, u32[]{:S(2)}, u32[]{:S(2)}) %all-to-all-start.1) | async-done | bytes 1572896 | tf_op jit(solution)/shard_map/all_to_all | solution.py:31
  100.7 1.3 copy.25
  101.9 12.3 %fusion.9 = bf16[2,192,3072]{2,1,0:T(8,128)(2,1)} fusion(f32[2]{0:T(128)S(1)} %dynamic_slice.3, f32[1024,3072]{0,1:T(8,128)} %get-tuple-element.6, f32[1024,3072]{0,1:T(8,128)} %get-tuple-element.5, bf16[16,2,24,8,128]{4,3,2,1,0:T(8,128)(2,1)} %bitcast.101), kind=kOutput, calls=%fused_computation.15 | convolution fusion | flops 4855431168 | bytes 29097992 | tf_op jit(solution)/shard_map/fyk,kx->fyx/dot_general | solution.py:73
  114.3 13.9 %convolution_convert_fusion.1 = bf16[2,192,2048]{2,1,0:T(8,128)(2,1)S(1)} fusion(bf16[2,192,3072]{2,1,0:T(8,128)(2,1)} %fusion.9, f32[1024,3072]{0,1:T(8,128)} %get-tuple-element.6, f32[1024,3072]{0,1:T(8,128)} %get-tuple-element.5), kind=kOutput, calls=%fused_computation.17 | convolution fusion | flops 4851499008 | bytes 29097984 | tf_op jit(solution)/shard_map/fyx,xk->fyk/dot_general | solution.py:75
  128.2 0.7 fusion.34
  128.8 0.7 fusion.33
  129.5 0.7 fusion.32
  130.2 0.7 fusion.31
  130.8 0.7 fusion.30
  131.5 0.7 fusion.29
  132.2 0.7 fusion.28
  132.8 0.7 fusion.27
  133.5 0.7 fusion.26
  134.2 0.7 fusion.25
  134.8 0.7 fusion.24
  135.5 0.7 fusion.23
  136.2 0.7 fusion.22
  136.8 0.7 fusion.21
  137.5 0.7 fusion.20
  138.2 0.7 fusion.19
  138.8 4.6 %all-to-all-start.2 = ((bf16[16,2,192,128]{3,2,1,0:T(8,128)(2,1)}), bf16[16,2,192,128]{3,2,1,0:T(8,128)(2,1)S(1)}, u32[]{:S(2)}, u32[]{:S(2)}) async-start(bf16[16,2,192,128]{3,2,1,0:T(8,128)(2,1)} %fusion.19), calls=%async_computation.2 | async-start | bytes 3145728 | tf_op jit(solution)/shard_map/all_to_all | solution.py:83
  143.5 1.1 fusion.18
  144.6 21.7 %all-to-all-done.2 = bf16[16,2,192,128]{3,2,1,0:T(8,128)(2,1)S(1)} async-done(((bf16[16,2,192,128]{3,2,1,0:T(8,128)(2,1)}), bf16[16,2,192,128]{3,2,1,0:T(8,128)(2,1)S(1)}, u32[]{:S(2)}, u32[]{:S(2)}) %all-to-all-start.2) | async-done | bytes 1572896 | tf_op jit(solution)/shard_map/all_to_all | solution.py:83
  166.3 1.3 copy.29
  167.7 12.3 %fusion.11 = bf16[2,2048,128]{1,2,0:T(8,128)(2,1)S(1)} fusion(bf16[2,3072,128]{2,1,0:T(8,128)(2,1)} %bitcast.100, f32[1024,3072]{0,1:T(8,128)} %get-tuple-element.6, f32[1024,3072]{0,1:T(8,128)} %get-tuple-element.5, f32[2048,128]{0,1:T(8,128)} %fusion.18), kind=kOutput, calls=%fused_computation.20 | convolution fusion | flops 3241148416 | bytes 28835840 | tf_op jit(solution)/shard_map/ky,fyc->fkc/dot_general | solution.py:87
  180.0 1.3 copy.32
  (3 shorter events, 0.0 us)
Async XLA Ops:
  0.0 52.6 %copy-start = (bf16[2,2048,128]{2,1,0:T(8,128)(2,1)S(1)}, bf16[2,2048,128]{2,1,0:T(8,128)(2,1)}, u32[]{:S(2)}) copy-start(bf16[2,2048,128]{2,1,0:T(8,128)(2,1)} %param.2) | copy-start | bytes 3145732
  70.1 7.6 %copy-start.1 = (f32[16]{0:T(128)S(1)}, f32[16]{0:T(128)}, u32[]{:S(2)}) copy-start(f32[16]{0:T(128)} %param.3) | copy-start | bytes 196
  70.1 30.6 %all-to-all-start.1 = ((bf16[8,2,2,192,128]{4,3,1,2,0:T(8,128)(2,1)}), bf16[8,2,2,192,128]{4,3,1,2,0:T(8,128)(2,1)S(1)}, u32[]{:S(2)}, u32[]{:S(2)}) async-start(bf16[8,2,2,192,128]{4,3,1,2,0:T(8,128)(2,1)} %copy.24), calls=%async_computation.1 | async-start | bytes 3145728 | tf_op jit(solution)/shard_map/all_to_all | solution.py:31
  138.8 27.5 %all-to-all-start.2 = ((bf16[16,2,192,128]{3,2,1,0:T(8,128)(2,1)}), bf16[16,2,192,128]{3,2,1,0:T(8,128)(2,1)S(1)}, u32[]{:S(2)}, u32[]{:S(2)}) async-start(bf16[16,2,192,128]{3,2,1,0:T(8,128)(2,1)} %fusion.19), calls=%async_computation.2 | async-start | bytes 3145728 | tf_op jit(solution)/shard_map/all_to_all | solution.py:83
